TPU v7x, 32 devices: a whole 2x2x4 slice. The times are simulated.
32 devices in a mesh: rows: 32 (over z, y, x, core).
Axes of the slice: x: 2, y: 2, z: 4, core: 2. Of those that a mesh axis runs over, the one named last changes fastest.
Arguments:
- source: float32 [64, 131072], P(None, 'rows'), may hold values from -6 to 6
- band_values: float32 [128, 131072], P(None, 'rows'), may hold values from -0.625 to 0.625
- offsets: int32 [128], replicated, may hold values from -128 to 128, as said below
Outputs:
- compressed: float32 [128, 131072], P(None, 'rows')
Inputs may be any that keep to these rules, and one draw needn't show every extreme that they name: The 128 offsets are distinct and include both -128 and 128.
All inputs are finite; a program needn't handle non-finite values.
Results may differ from a plain program's by a relative error of at most 0.0003.
Values sent between devices are 32-bit elements; how exact they have to be, the bound alone decides.
A program may use at most 192 MiB of HBM per device.

v0:
```python
import jax
import jax.numpy as jnp
from jax import lax
from jax.sharding import PartitionSpec as P

HB = 128
K2 = 128


def padded(block, sides, width):
    for axis, dim in sides:
        count = lax.axis_size(axis)
        forward = [(i, i + 1) for i in range(count - 1)]
        backward = [(target, source) for source, target in forward]
        low = lax.ppermute(
            lax.slice_in_dim(block, block.shape[dim] - width, None, axis=dim), axis, forward
        )
        high = lax.ppermute(lax.slice_in_dim(block, 0, width, axis=dim), axis, backward)
        block = jnp.concatenate([low, block, high], axis=dim)
    return block


def band_blocks(band_values, offsets):
    diagonals = band_values.shape[0]
    blocks = band_values.shape[1] // HB
    values = band_values.reshape(diagonals, blocks, HB).transpose(1, 0, 2)
    within = jnp.arange(HB, dtype=jnp.int32)
    columns = within[None, :] + offsets[:, None] + HB
    row_index = jnp.broadcast_to(within[None, :], columns.shape)
    blocked = jnp.zeros((blocks, HB, 3 * HB), values.dtype)
    return blocked.at[:, row_index, columns].set(values)


def apply_band(extended, blocked):
    width = extended.shape[0]
    blocks = blocked.shape[0]
    pieces = extended.reshape(width, blocks + 2, HB)
    windows = jnp.concatenate([pieces[:, :-2], pieces[:, 1:-1], pieces[:, 2:]], axis=2)
    result = jnp.einsum("cbj,brj->cbr", windows, blocked, precision=lax.Precision.HIGHEST)
    return result.reshape(width, blocks * HB)


def compress(grammian, retain):
    spanning = grammian[:, :retain]
    coeffs = None
    for repeat in range(2):
        if repeat > 0:
            spanning = jnp.dot(grammian, coeffs.T, precision=lax.Precision.HIGHEST)
        mapped = jnp.dot(grammian, spanning, precision=lax.Precision.HIGHEST)
        metric = jnp.dot(spanning.T, mapped, precision=lax.Precision.HIGHEST)
        metric = 0.5 * (metric + metric.T)
        factor = jnp.linalg.cholesky(metric)
        coeffs = jax.scipy.linalg.solve_triangular(factor, spanning.T, lower=True)
    return coeffs


def gram_total(stacked, total):
    local = jnp.dot(stacked, stacked.T, precision=lax.Precision.HIGHEST)
    summed = lax.psum(local, "rows")
    return summed / total


def first_gram(first, total):
    return gram_total(first, total)


def second_gram(factor, squared, total):
    return gram_total(jnp.concatenate([factor, squared], axis=0), total)


def body(source, band_values, offsets):
    devices_here = lax.axis_size("rows")
    total = float(source.shape[1] * devices_here)
    keep_first = 2 * source.shape[0]
    deep_source = padded(source, (("rows", 1),), 3 * HB)
    deep_band = padded(band_values, (("rows", 1),), 2 * HB)
    blocked = band_blocks(deep_band, offsets)
    first_deep = jnp.concatenate([deep_source[:, HB:-HB], apply_band(deep_source, blocked)], axis=0)
    first = first_deep[:, 2 * HB : -2 * HB]
    gram_one = first_gram(first, total)
    coeffs_one = compress(gram_one, keep_first)
    factor_deep = jnp.dot(coeffs_one, first_deep, precision=lax.Precision.HIGHEST)
    factor = factor_deep[:, 2 * HB : -2 * HB]
    once_more = apply_band(factor_deep, blocked[1:-1])
    squared = apply_band(once_more, blocked[2:-2])
    second = jnp.concatenate([factor, squared], axis=0)
    coeffs_two = compress(second_gram(factor, squared, total), K2)
    return jnp.dot(coeffs_two, second, precision=lax.Precision.HIGHEST)


def solution(mesh):
    placed = (P(None, "rows"), P(None, "rows"), P())
    return jax.shard_map(
        body, mesh=mesh, in_specs=placed, out_specs=P(None, "rows"), check_vma=False
    )
```

profile of v0, /device:TPU:0, one launch (start us, length us, event | category | flops | bytes accessed | tf_op | source)
XLA Modules:
  0.0 541.9 jit_solution(10150455950687637669)
XLA Ops:
  6.6 2.0 copy.71
  8.6 0.7 fusion.101
  9.3 1.3 collective-permute-start.3
  10.6 3.7 collective-permute-start.2
  14.3 3.9 collective-permute-start
  18.2 1.3 collective-permute-start.1
  19.8 0.6 select_bitcast_fusion
  20.4 0.6 constant_dynamic-update-slice_fusion.2
  21.1 1.0 constant_dynamic-update-slice_fusion.1
  22.1 0.6 constant_dynamic-update-slice_fusion
  22.8 1.5 reshape.80
  24.5 1.4 slice.90
  25.9 1.2 copy.105
  27.1 1.2 copy.104
  28.3 1.2 copy.103
  29.6 2.5 pad_maximum_fusion.3
  32.0 8.6 %copy.98 = f32[128,128,36]{2,1,0:T(8,128)} copy(f32[128,128,36]{0,1,2:T(8,128)} %bitcast.109) | data formatting | bytes 4718592 | tf_op jit(solution)/shard_map/transpose | solution.py:26
  40.6 51.0 %scatter_custom_fusion = f32[36,49152]{0,1:T(8,128)} fusion(s32[16384]{0:T(1024)} %select_bitcast_fusion, f32[16384,36]{1,0:T(8,128)} %bitcast.111, f32[]{:T(128)} %constant.47.clone.1), kind=kCustom, calls=%fused_computation.1 | custom fusion | bytes 7078400
  91.7 17.8 %copy.79 = f32[36,128,384]{2,1,0:T(8,128)} copy(f32[36,128,384]{0,2,1:T(8,128)} %bitcast.101) | data formatting | bytes 14155776 | tf_op jit(solution)/shard_map/scatter | solution.py:31
  109.5 12.0 %fusion.33 = f32[36,8,8,128]{3,2,1,0:T(8,128)S(1)} fusion(f32[36,128,384]{2,1,0:T(8,128)} %copy.79, f32[64,36,128]{2,0,1:T(8,128)S(1)} %copy-done.2, f32[64,36,128]{2,0,1:T(8,128)S(1)} %copy-done.3, f32[64,36,128]{2,0,1:T(8,128)} %copy.103), kind=kOutput, calls=%fused_computation.34 | convolution fusion | flops 1360723968 | bytes 11796480 | tf_op jit(solution)/shard_map/cbj,brj->cbr/dot_general | solution.py:39
  121.5 2.4 fusion.26
  124.0 18.9 %slice.97 = f32[32,49152]{0,1:T(8,128)} slice(f32[36,49152]{0,1:T(8,128)} %scatter_custom_fusion), slice={[2:34], [0:49152]} | slice | bytes 12582912 | tf_op jit(solution)/shard_map/slice | solution.py:85
  143.0 19.0 %slice.98 = f32[34,49152]{0,1:T(8,128)} slice(f32[36,49152]{0,1:T(8,128)} %scatter_custom_fusion), slice={[1:35], [0:49152]} | slice | bytes 13369344 | tf_op jit(solution)/shard_map/slice | solution.py:84
  162.0 17.2 %copy.99 = f32[32,128,384]{2,1,0:T(8,128)} copy(f32[32,128,384]{0,2,1:T(8,128)} %bitcast.103) | data formatting | bytes 12582912 | tf_op jit(solution)/shard_map/slice | solution.py:85
  179.2 17.7 %copy.100 = f32[34,128,384]{2,1,0:T(8,128)} copy(f32[34,128,384]{0,2,1:T(8,128)} %bitcast.102) | data formatting | bytes 13369344 | tf_op jit(solution)/shard_map/slice | solution.py:84
  196.9 52.0 %all-reduce.3.cloned.1.call-done = f32[128,128]{1,0:T(8,128)} async-done(((f32[128,128]{1,0:T(8,128)}), f32[128,128]{1,0:T(8,128)}) %all-reduce.3.cloned.1.call-update) | async-done | bytes 65552 | tf_op jit(solution)/shard_map/psum | solution.py:59
  249.0 1.1 fusion.78
  250.1 1.1 fusion.76
  251.4 11.7 %cholesky.74 = f32[128,128]{1,0:T(8,128)S(1)} custom-call(f32[128,128]{1,0:T(8,128)S(1)} %fusion.63), custom_call_target="Cholesky" | custom-call | tf_op jit(solution)/shard_map/jit(cholesky)/cholesky | solution.py:52
  263.2 0.6 compare_reduce_fusion.3
  263.8 0.7 fusion.45
  264.5 9.8 %custom-call.10 = f32[1,128,128]{1,2,0:T(8,128)S(1)} custom-call(f32[1,128,128]{2,1,0:T(8,128)S(1)} %fusion.45), custom_call_target="InvertDiagBlocksLowerTriangular" | custom-call | tf_op jit(solution)/shard_map/jit(_solve_triangular)/triangular_solve | solution.py:53
  274.3 1.1 fusion.60
  275.4 1.1 fusion.73
  276.6 1.0 fusion.71
  278.1 11.7 %cholesky.85 = f32[128,128]{1,0:T(8,128)S(1)} custom-call(f32[128,128]{1,0:T(8,128)S(1)} %fusion.58), custom_call_target="Cholesky" | custom-call | tf_op jit(solution)/shard_map/jit(cholesky)/cholesky | solution.py:52
  289.9 0.6 compare_reduce_fusion.2
  290.5 0.7 fusion.46
  291.2 10.2 %custom-call.11 = f32[1,128,128]{1,2,0:T(8,128)S(1)} custom-call(f32[1,128,128]{2,1,0:T(8,128)S(1)} %fusion.46), custom_call_target="InvertDiagBlocksLowerTriangular" | custom-call | tf_op jit(solution)/shard_map/jit(_solve_triangular)/triangular_solve | solution.py:53
  301.7 3.5 fusion.22
  305.2 2.0 copy.87
  307.2 3.2 slice.96
  310.4 2.9 fusion.99
  313.3 3.1 copy.108
  316.5 1.9 copy.107
  318.4 3.2 copy.106
  321.5 11.8 %fusion.30 = f32[128,34,128]{0,2,1:T(8,128)S(1)} fusion(f32[34,128,384]{2,1,0:T(8,128)} %copy.100, f32[128,34,128]{2,0,1:T(8,128)} %copy.108, f32[128,34,128]{2,0,1:T(8,128)} %copy.107, f32[128,34,128]{2,0,1:T(8,128)} %copy.106), kind=kOutput, calls=%fused_computation.33 | convolution fusion | flops 2570256384 | bytes 15597568 | tf_op jit(solution)/shard_map/cbj,brj->cbr/dot_general | solution.py:39
  333.3 0.8 fusion.100
  334.1 7.7 %fusion.8 = f32[32,128,128]{2,1,0:T(8,128)} fusion(f32[32,128,384]{2,1,0:T(8,128)S(1)} %bitcast.106, f32[128,32,128]{0,2,1:T(8,128)S(1)} %get-tuple-element.12, f32[128,32,128]{0,2,1:T(8,128)S(1)} %get-tuple-element.13, f32[128,32,128]{0,2,1:T(8,128)S(1)} %get-tuple-element.11), kind=kOutput, calls=%fused_computation.9 | convolution fusion | flops 2419064832 | bytes 14680064 | tf_op jit(solution)/shard_map/cbj,brj->cbr/dot_general | solution.py:39
  341.9 3.2 copy.101
  345.1 6.5 %fusion.21 = f32[256,256]{1,0:T(8,128)} fusion(f32[128,4096]{1,0:T(8,128)} %copy.101, f32[128,4096]{1,0:T(8,128)S(1)} %copy-done.1), kind=kOutput, calls=%fused_computation.23 | convolution fusion | flops 3222274048 | bytes 4456448 | tf_op jit(solution)/shard_map/dot_general | solution.py:58
  351.6 128.0 %all-reduce.5.cloned.1.call-done = f32[256,256]{1,0:T(8,128)} async-done(((f32[256,256]{1,0:T(8,128)}), f32[256,256]{1,0:T(8,128)}) %all-reduce.5.cloned.1.call-update) | async-done | bytes 262160 | tf_op jit(solution)/shard_map/psum | solution.py:59
  479.6 1.0 broadcast_multiply_fusion
  481.0 0.4 fusion.41
  481.6 11.7 %cholesky.96 = f32[128,128]{1,0:T(8,128)S(1)} custom-call(f32[128,128]{1,0:T(8,128)S(1)} %fusion.53), custom_call_target="Cholesky" | custom-call | tf_op jit(solution)/shard_map/jit(cholesky)/cholesky | solution.py:52
  493.4 0.6 compare_reduce_fusion.1
  494.0 0.7 fusion.47
  494.7 9.8 %custom-call.12 = f32[1,128,128]{1,2,0:T(8,128)S(1)} custom-call(f32[1,128,128]{2,1,0:T(8,128)S(1)} %fusion.47), custom_call_target="InvertDiagBlocksLowerTriangular" | custom-call | tf_op jit(solution)/shard_map/jit(_solve_triangular)/triangular_solve | solution.py:53
  505.6 0.4 fusion.105
  506.2 11.9 %cholesky.107 = f32[128,128]{1,0:T(8,128)S(1)} custom-call(f32[128,128]{1,0:T(8,128)S(1)} %fusion.50), custom_call_target="Cholesky" | custom-call | tf_op jit(solution)/shard_map/jit(cholesky)/cholesky | solution.py:52
  518.1 0.6 compare_reduce_fusion
  518.8 0.7 fusion.48
  519.5 9.8 %custom-call.13 = f32[1,128,128]{1,2,0:T(8,128)S(1)} custom-call(f32[1,128,128]{2,1,0:T(8,128)S(1)} %fusion.48), custom_call_target="InvertDiagBlocksLowerTriangular" | custom-call | tf_op jit(solution)/shard_map/jit(_solve_triangular)/triangular_solve | solution.py:53
  529.6 5.2 fusion.20
  (65 shorter events, 4.0 us)
Async XLA Ops:
  6.5 13.0 %copy-start.7 = (s32[2]{0:T(128)S(1)}, s32[2]{0:T(128)}, u32[]{:S(2)}) copy-start(s32[2]{0:T(128)} %constant.56) | copy-start | bytes 28
  6.5 13.2 %copy-start.8 = (s32[2]{0:T(128)S(1)}, s32[2]{0:T(128)}, u32[]{:S(2)}) copy-start(s32[2]{0:T(128)} %constant.53) | copy-start | bytes 28
  6.5 7.7 %copy-start.5 = (f32[64,4096]{1,0:T(8,128)S(1)}, f32[64,4096]{1,0:T(8,128)}, u32[]{:S(2)}) copy-start(f32[64,4096]{1,0:T(8,128)} %param.8) | copy-start | bytes 3145732
  6.5 12.9 %copy-start.6 = (s32[128]{0:T(128)S(1)}, s32[128]{0:T(128)}, u32[]{:S(2)}) copy-start(s32[128]{0:T(128)} %param.10) | copy-start | bytes 1540
  6.5 242.4 %all-reduce.3.cloned.1.call-start = ((), (), s32[]{:S(2)}) async-start(), calls=%async_computation | async-start | bytes 131072 | tf_op jit(solution)/shard_map/psum | solution.py:59
  9.3 20.3 %collective-permute-start.3 = (f32[128,256]{0,1:T(8,128)}, f32[128,256]{0,1:T(8,128)S(1)}, u32[]{:S(2)}, u32[]{:S(2)}) collective-permute-start(f32[128,256]{0,1:T(8,128)} %get-tuple-element.15), channel_id=1, source_target_pairs={{1,0},{2,1},{3,2},{4,3},{5,4},{6,5},{7,6},{8,7},{9,8},{10,9},{11,1... | collective-permute-start | bytes 393224 | tf_op jit(solution)/shard_map/ppermute | solution.py:18
  10.6 19.0 %collective-permute-start.2 = (f32[128,256]{0,1:T(8,128)}, f32[128,256]{0,1:T(8,128)}, u32[]{:S(2)}, u32[]{:S(2)}) collective-permute-start(f32[128,256]{0,1:T(8,128)} %get-tuple-element.14), channel_id=1, source_target_pairs={{0,1},{1,2},{2,3},{3,4},{4,5},{5,6},{6,7},{7,8},{8,9},{9,10},{10,1... | collective-permute-start | bytes 393224 | tf_op jit(solution)/shard_map/ppermute | solution.py:15
  14.3 6.1 %collective-permute-start = (f32[64,384]{1,0:T(8,128)S(1)}, f32[64,384]{1,0:T(8,128)S(1)}, u32[]{:S(2)}, u32[]{:S(2)}) collective-permute-start(f32[64,384]{1,0:T(8,128)S(1)} %get-tuple-element.20), channel_id=1, source_target_pairs={{0,1},{1,2},{2,3},{3,4},{4,5},{5,6},{6,7},{7,8},{8,9},{9,10},{10,1... | collective-permute-start | bytes 294920 | tf_op jit(solution)/shard_map/ppermute | solution.py:15
  18.2 3.9 collective-permute-start.1
  91.7 17.8 %copy-start.2 = (f32[64,36,128]{2,0,1:T(8,128)S(1)}, f32[64,36,128]{2,0,1:T(8,128)}, u32[]{:S(2)}) copy-start(f32[64,36,128]{2,0,1:T(8,128)} %copy.105) | copy-start | bytes 3538948
  91.7 17.8 %copy-start.3 = (f32[64,36,128]{2,0,1:T(8,128)S(1)}, f32[64,36,128]{2,0,1:T(8,128)}, u32[]{:S(2)}) copy-start(f32[64,36,128]{2,0,1:T(8,128)} %copy.104) | copy-start | bytes 3538948
  124.0 355.6 %all-reduce.5.cloned.1.call-start = ((), (), s32[]{:S(2)}) async-start(), calls=%async_computation.1 | async-start | bytes 524288 | tf_op jit(solution)/shard_map/psum | solution.py:59
  313.3 3.1 copy-start
  318.4 15.7 %slice-start = ((s8[6291456]{0:T(1024)(128)(4,1)}), s8[2097152]{0:T(1024)(128)(4,1)S(1)}, s32[]{:S(2)}) async-start(s8[6291456]{0:T(1024)(128)(4,1)} %bitcast.105), calls=%async_computation.2 | async-start | bytes 4194304
  321.5 12.6 %slice-start.1 = ((s8[6291456]{0:T(1024)(128)(4,1)}), s8[4194304]{0:T(1024)(128)(4,1)S(1)}, s32[]{:S(2)}) async-start(s8[6291456]{0:T(1024)(128)(4,1)} %bitcast.105), calls=%async_computation.3 | async-start | bytes 8388608
  341.9 3.2 copy-start.1
  479.6 25.2 %copy-start.4 = (f32[256,256]{1,0:T(8,128)S(1)}, f32[256,256]{1,0:T(8,128)}, u32[]{:S(2)}) copy-start(f32[256,256]{1,0:T(8,128)} %all-reduce.5.cloned.1.call-done) | copy-start | bytes 786436
Sparse Core Ops, SparseCore 0:
  124.1 124.8 all-reduce.2
  351.7 127.8 all-reduce.4
where the time goes:
time: 549 us; the launch traced here: 542 us
  local copies, waits for them, and re-layouts  183 us (33%)
  waiting for transfers between devices  180 us (33%)
  other arithmetic  96.5 us (18%)
  matrix products  57.7 us (11%)
  between operations  14.2 us (3%)
  starting transfers between devices  10.2 us (2%)
    psum x2, waiting for transfers between devices, gram_total(): summed = lax.psum(local, 'rows')  180 us
    unnamed x32, local copies, waits for them, and re-layouts  66.7 us
    another operation x12, other arithmetic, compress(): factor = jnp.linalg.cholesky(metric)  49.7 us
    another operation x8, other arithmetic, compress(): coeffs = jax.scipy.linalg.solve_triangular(factor, spanning.T, lower=True)  42.2 us
    slice x2, local copies, waits for them, and re-layouts, body(): once_more = apply_band(factor_deep, blocked[1:-1])  36.8 us
    slice x2, local copies, waits for them, and re-layouts, body(): squared = apply_band(once_more, blocked[2:-2])  36.1 us
    dot_general x3, matrix products, apply_band(): jnp.einsum('cbj,brj->cbr', windows, blocked, precision=lax.Precision.HIGH...  31.5 us
    scatter x1, local copies, waits for them, and re-layouts, band_blocks(): return blocked.at[:, row_index, columns].set(values)  17.8 us
  transfers between devices with their start and end apart: 6, of which 2 were waited for; matrix products, arithmetic and copies ran while one was open for 15% of the time, Pallas kernels for 0%

commit v1 on v0

--- a/solution.py
+++ b/solution.py
@@ -56,7 +56,7 @@
 
 def gram_total(stacked, total):
     local = jnp.dot(stacked, stacked.T, precision=lax.Precision.HIGHEST)
-    summed = lax.psum(local, "rows")
+    summed = jnp.sum(lax.all_gather(local, "rows"), axis=0)
     return summed / total
 
 

time: 549 us -> 452 us (0.82)
  waiting for transfers between devices: 180 us -> 82.8 us
    psum x2 -> x0, waiting for transfers between devices: 180 us -> none  [gram_total(): summed = lax.psum(local, 'rows')]
    all_gather x0 -> x2, waiting for transfers between devices: none -> 82.8 us  [gram_total(): summed = jnp.sum(lax.all_gather(local, 'rows'), axis=0)]
    reduce_sum x0 -> x2, other arithmetic: none -> 5.63 us  [gram_total(): summed = jnp.sum(lax.all_gather(local, 'rows'), axis=0)]
    unnamed x32 -> x30, local copies, waits for them, and re-layouts: 66.7 us -> 66.7 us
  transfers between devices with their start and end apart: 6 -> 6, of which waited for: 2 -> 1; matrix products, arithmetic and copies ran while one was open for 15% -> 19% of each run, Pallas kernels for 0% -> 0%
where the time goes in v1:
time: 452 us; the launch traced here: 445 us
  local copies, waits for them, and re-layouts  183 us (40%)
  other arithmetic  101 us (22%)
  waiting for transfers between devices  82.8 us (18%)
  matrix products  53.7 us (12%)
  between operations  14.2 us (3%)
  starting transfers between devices  10.2 us (2%)
    all_gather x2, waiting for transfers between devices, gram_total(): summed = jnp.sum(lax.all_gather(local, 'rows'), axis=0)  82.8 us
    unnamed x30, local copies, waits for them, and re-layouts  66.7 us
    another operation x12, other arithmetic, compress(): factor = jnp.linalg.cholesky(metric)  49.6 us
    another operation x8, other arithmetic, compress(): coeffs = jax.scipy.linalg.solve_triangular(factor, spanning.T, lower=True)  42.2 us
    slice x2, local copies, waits for them, and re-layouts, body(): once_more = apply_band(factor_deep, blocked[1:-1])  36.6 us
    slice x2, local copies, waits for them, and re-layouts, body(): squared = apply_band(once_more, blocked[2:-2])  36.3 us
    dot_general x3, matrix products, apply_band(): jnp.einsum('cbj,brj->cbr', windows, blocked, precision=lax.Precision.HIGH...  31.5 us
    scatter x1, local copies, waits for them, and re-layouts, band_blocks(): return blocked.at[:, row_index, columns].set(values)  17.8 us
  transfers between devices with their start and end apart: 6, of which 1 were waited for; matrix products, arithmetic and copies ran while one was open for 19% of the time, Pallas kernels for 0%

profile of v1, /device:TPU:0, one launch (start us, length us, event | category | flops | bytes accessed | tf_op | source)
XLA Modules:
  0.0 445.0 jit_solution(2475284802687087528)
XLA Ops:
  6.6 2.0 copy.71
  8.6 0.7 fusion.101
  9.3 1.3 collective-permute-start.3
  10.6 3.7 collective-permute-start.2
  14.3 3.9 collective-permute-start
  18.2 1.3 collective-permute-start.1
  19.8 0.6 select_bitcast_fusion
  20.4 0.6 constant_dynamic-update-slice_fusion.2
  21.1 1.0 constant_dynamic-update-slice_fusion.1
  22.1 0.6 constant_dynamic-update-slice_fusion
  22.8 1.5 reshape.80
  24.5 1.4 slice.90
  25.9 1.2 copy.105
  27.1 1.2 copy.104
  28.3 1.2 copy.103
  29.6 2.5 pad_maximum_fusion.3
  32.0 8.6 %copy.98 = f32[128,128,36]{2,1,0:T(8,128)} copy(f32[128,128,36]{0,1,2:T(8,128)} %bitcast.111) | data formatting | bytes 4718592 | tf_op jit(solution)/shard_map/transpose | solution.py:26
  40.6 51.0 %scatter_custom_fusion = f32[36,49152]{0,1:T(8,128)} fusion(s32[16384]{0:T(1024)} %select_bitcast_fusion, f32[16384,36]{1,0:T(8,128)} %bitcast.114, f32[]{:T(128)} %constant.48.clone.1), kind=kCustom, calls=%fused_computation.1 | custom fusion | bytes 7078400
  91.7 17.8 %copy.79 = f32[36,128,384]{2,1,0:T(8,128)} copy(f32[36,128,384]{0,2,1:T(8,128)} %bitcast.103) | data formatting | bytes 14155776 | tf_op jit(solution)/shard_map/scatter | solution.py:31
  109.5 12.0 %fusion.33 = f32[36,8,8,128]{3,2,1,0:T(8,128)S(1)} fusion(f32[36,128,384]{2,1,0:T(8,128)} %copy.79, f32[64,36,128]{2,0,1:T(8,128)S(1)} %copy-done.2, f32[64,36,128]{2,0,1:T(8,128)S(1)} %copy-done.3, f32[64,36,128]{2,0,1:T(8,128)} %copy.103), kind=kOutput, calls=%fused_computation.34 | convolution fusion | flops 1360723968 | bytes 11796480 | tf_op jit(solution)/shard_map/cbj,brj->cbr/dot_general | solution.py:39
  121.5 2.4 fusion.26
  124.0 19.0 %slice.97 = f32[32,49152]{0,1:T(8,128)} slice(f32[36,49152]{0,1:T(8,128)} %scatter_custom_fusion), slice={[2:34], [0:49152]} | slice | bytes 12582912 | tf_op jit(solution)/shard_map/slice | solution.py:85
  143.0 19.0 %slice.98 = f32[34,49152]{0,1:T(8,128)} slice(f32[36,49152]{0,1:T(8,128)} %scatter_custom_fusion), slice={[1:35], [0:49152]} | slice | bytes 13369344 | tf_op jit(solution)/shard_map/slice | solution.py:84
  162.0 17.3 %copy.99 = f32[32,128,384]{2,1,0:T(8,128)} copy(f32[32,128,384]{0,2,1:T(8,128)} %bitcast.105) | data formatting | bytes 12582912 | tf_op jit(solution)/shard_map/slice | solution.py:85
  179.3 17.6 %copy.100 = f32[34,128,384]{2,1,0:T(8,128)} copy(f32[34,128,384]{0,2,1:T(8,128)} %bitcast.104) | data formatting | bytes 13369344 | tf_op jit(solution)/shard_map/slice | solution.py:84
  196.9 1.7 reduce_sum.18
  199.4 11.7 %cholesky.74 = f32[128,128]{1,0:T(8,128)S(1)} custom-call(f32[128,128]{1,0:T(8,128)S(1)} %fusion.63), custom_call_target="Cholesky" | custom-call | tf_op jit(solution)/shard_map/jit(cholesky)/cholesky | solution.py:52
  211.1 0.6 compare_reduce_fusion.3
  211.8 0.7 fusion.45
  212.4 9.8 %custom-call.10 = f32[1,128,128]{1,2,0:T(8,128)S(1)} custom-call(f32[1,128,128]{2,1,0:T(8,128)S(1)} %fusion.45), custom_call_target="InvertDiagBlocksLowerTriangular" | custom-call | tf_op jit(solution)/shard_map/jit(_solve_triangular)/triangular_solve | solution.py:53
  223.5 11.7 %cholesky.85 = f32[128,128]{1,0:T(8,128)S(1)} custom-call(f32[128,128]{1,0:T(8,128)S(1)} %fusion.58), custom_call_target="Cholesky" | custom-call | tf_op jit(solution)/shard_map/jit(cholesky)/cholesky | solution.py:52
  235.3 0.6 compare_reduce_fusion.2
  235.9 0.7 fusion.46
  236.6 10.2 %custom-call.11 = f32[1,128,128]{1,2,0:T(8,128)S(1)} custom-call(f32[1,128,128]{2,1,0:T(8,128)S(1)} %fusion.46), custom_call_target="InvertDiagBlocksLowerTriangular" | custom-call | tf_op jit(solution)/shard_map/jit(_solve_triangular)/triangular_solve | solution.py:53
  247.1 3.5 fusion.22
  250.6 2.0 copy.87
  252.6 3.2 slice.96
  255.8 2.9 fusion.99
  258.7 3.1 copy.108
  261.9 1.9 copy.107
  263.8 3.2 copy.106
  267.0 11.8 %fusion.30 = f32[128,34,128]{0,2,1:T(8,128)S(1)} fusion(f32[34,128,384]{2,1,0:T(8,128)} %copy.100, f32[128,34,128]{2,0,1:T(8,128)} %copy.108, f32[128,34,128]{2,0,1:T(8,128)} %copy.107, f32[128,34,128]{2,0,1:T(8,128)} %copy.106), kind=kOutput, calls=%fused_computation.33 | convolution fusion | flops 2570256384 | bytes 15597568 | tf_op jit(solution)/shard_map/cbj,brj->cbr/dot_general | solution.py:39
  278.7 0.8 fusion.100
  279.5 7.7 %fusion.8 = f32[32,128,128]{2,1,0:T(8,128)} fusion(f32[32,128,384]{2,1,0:T(8,128)S(1)} %bitcast.108, f32[128,32,128]{0,2,1:T(8,128)S(1)} %get-tuple-element.12, f32[128,32,128]{0,2,1:T(8,128)S(1)} %get-tuple-element.13, f32[128,32,128]{0,2,1:T(8,128)S(1)} %get-tuple-element.11), kind=kOutput, calls=%fused_computation.9 | convolution fusion | flops 2419064832 | bytes 14680064 | tf_op jit(solution)/shard_map/cbj,brj->cbr/dot_general | solution.py:39
  287.3 3.3 copy.101
  290.5 6.5 %fusion.21 = f32[256,256]{1,0:T(8,128)} fusion(f32[128,4096]{1,0:T(8,128)} %copy.101, f32[128,4096]{1,0:T(8,128)S(1)} %copy-done.1), kind=kOutput, calls=%fused_computation.23 | convolution fusion | flops 3222274048 | bytes 4456448 | tf_op jit(solution)/shard_map/dot_general | solution.py:58
  297.1 82.8 %all-gather.7.cloned.1.call-done = f32[8192,256]{1,0:T(8,128)} async-done(((f32[256,256]{1,0:T(8,128)}), f32[8192,256]{1,0:T(8,128)}) %all-gather.7.cloned.1.call-update) | async-done | bytes 8388624 | tf_op jit(solution)/shard_map/all_gather | solution.py:59
  379.8 3.9 reduce_sum.19
  383.8 0.4 fusion.43
  384.2 0.4 fusion.41
  384.8 11.7 %cholesky.96 = f32[128,128]{1,0:T(8,128)S(1)} custom-call(f32[128,128]{1,0:T(8,128)S(1)} %fusion.53), custom_call_target="Cholesky" | custom-call | tf_op jit(solution)/shard_map/jit(cholesky)/cholesky | solution.py:52
  396.5 0.6 compare_reduce_fusion.1
  397.2 0.7 fusion.47
  397.8 9.8 %custom-call.12 = f32[1,128,128]{1,2,0:T(8,128)S(1)} custom-call(f32[1,128,128]{2,1,0:T(8,128)S(1)} %fusion.47), custom_call_target="InvertDiagBlocksLowerTriangular" | custom-call | tf_op jit(solution)/shard_map/jit(_solve_triangular)/triangular_solve | solution.py:53
  407.7 0.3 fusion.38
  408.0 0.4 fusion.98
  408.4 0.6 fusion.97
  409.0 0.4 fusion.105
  409.6 11.7 %cholesky.107 = f32[128,128]{1,0:T(8,128)S(1)} custom-call(f32[128,128]{1,0:T(8,128)S(1)} %fusion.50), custom_call_target="Cholesky" | custom-call | tf_op jit(solution)/shard_map/jit(cholesky)/cholesky | solution.py:52
  421.3 0.6 compare_reduce_fusion
  422.0 0.7 fusion.48
  422.6 9.8 %custom-call.13 = f32[1,128,128]{1,2,0:T(8,128)S(1)} custom-call(f32[1,128,128]{2,1,0:T(8,128)S(1)} %fusion.48), custom_call_target="InvertDiagBlocksLowerTriangular" | custom-call | tf_op jit(solution)/shard_map/jit(_solve_triangular)/triangular_solve | solution.py:53
  432.4 0.3 fusion.36
  432.8 5.2 %fusion.20 = f32[128,4096]{1,0:T(8,128)} fusion(f32[128,256]{1,0:T(8,128)S(1)} %fusion.36, f32[128,4096]{1,0:T(8,128)} %copy.101, f32[128,4096]{1,0:T(8,128)S(1)} %copy-done.1), kind=kOutput, calls=%fused_computation.22 | convolution fusion | flops 1611661312 | bytes 6422528 | tf_op jit(solution)/shard_map/dot_general | solution.py:88
  (65 shorter events, 3.6 us)
Async XLA Ops:
  6.5 13.0 %copy-start.6 = (s32[2]{0:T(128)S(1)}, s32[2]{0:T(128)}, u32[]{:S(2)}) copy-start(s32[2]{0:T(128)} %constant.57) | copy-start | bytes 28
  6.5 13.2 %copy-start.7 = (s32[2]{0:T(128)S(1)}, s32[2]{0:T(128)}, u32[]{:S(2)}) copy-start(s32[2]{0:T(128)} %constant.54) | copy-start | bytes 28
  6.5 7.7 %copy-start.4 = (f32[64,4096]{1,0:T(8,128)S(1)}, f32[64,4096]{1,0:T(8,128)}, u32[]{:S(2)}) copy-start(f32[64,4096]{1,0:T(8,128)} %param.8) | copy-start | bytes 3145732
  6.5 12.9 %copy-start.5 = (s32[128]{0:T(128)S(1)}, s32[128]{0:T(128)}, u32[]{:S(2)}) copy-start(s32[128]{0:T(128)} %param.10) | copy-start | bytes 1540
  6.5 190.4 %all-gather.5.cloned.1.call-start = ((), (), s32[]{:S(2)}) async-start(), calls=%async_computation | async-start | bytes 2162688 | tf_op jit(solution)/shard_map/all_gather | solution.py:59
  9.3 20.3 %collective-permute-start.3 = (f32[128,256]{0,1:T(8,128)}, f32[128,256]{0,1:T(8,128)S(1)}, u32[]{:S(2)}, u32[]{:S(2)}) collective-permute-start(f32[128,256]{0,1:T(8,128)} %get-tuple-element.15), channel_id=1, source_target_pairs={{1,0},{2,1},{3,2},{4,3},{5,4},{6,5},{7,6},{8,7},{9,8},{10,9},{11,1... | collective-permute-start | bytes 393224 | tf_op jit(solution)/shard_map/ppermute | solution.py:18
  10.6 19.0 %collective-permute-start.2 = (f32[128,256]{0,1:T(8,128)}, f32[128,256]{0,1:T(8,128)}, u32[]{:S(2)}, u32[]{:S(2)}) collective-permute-start(f32[128,256]{0,1:T(8,128)} %get-tuple-element.14), channel_id=1, source_target_pairs={{0,1},{1,2},{2,3},{3,4},{4,5},{5,6},{6,7},{7,8},{8,9},{9,10},{10,1... | collective-permute-start | bytes 393224 | tf_op jit(solution)/shard_map/ppermute | solution.py:15
  14.3 6.1 %collective-permute-start = (f32[64,384]{1,0:T(8,128)S(1)}, f32[64,384]{1,0:T(8,128)S(1)}, u32[]{:S(2)}, u32[]{:S(2)}) collective-permute-start(f32[64,384]{1,0:T(8,128)S(1)} %get-tuple-element.20), channel_id=1, source_target_pairs={{0,1},{1,2},{2,3},{3,4},{4,5},{5,6},{6,7},{7,8},{8,9},{9,10},{10,1... | collective-permute-start | bytes 294920 | tf_op jit(solution)/shard_map/ppermute | solution.py:15
  18.2 3.9 collective-permute-start.1
  91.7 17.8 %copy-start.2 = (f32[64,36,128]{2,0,1:T(8,128)S(1)}, f32[64,36,128]{2,0,1:T(8,128)}, u32[]{:S(2)}) copy-start(f32[64,36,128]{2,0,1:T(8,128)} %copy.105) | copy-start | bytes 3538948
  91.7 17.8 %copy-start.3 = (f32[64,36,128]{2,0,1:T(8,128)S(1)}, f32[64,36,128]{2,0,1:T(8,128)}, u32[]{:S(2)}) copy-start(f32[64,36,128]{2,0,1:T(8,128)} %copy.104) | copy-start | bytes 3538948
  124.0 255.8 %all-gather.7.cloned.1.call-start = ((), (), s32[]{:S(2)}) async-start(), calls=%async_computation.1 | async-start | bytes 8650752 | tf_op jit(solution)/shard_map/all_gather | solution.py:59
  258.7 3.1 copy-start
  263.8 15.7 %slice-start = ((s8[6291456]{0:T(1024)(128)(4,1)}), s8[2097152]{0:T(1024)(128)(4,1)S(1)}, s32[]{:S(2)}) async-start(s8[6291456]{0:T(1024)(128)(4,1)} %bitcast.107), calls=%async_computation.2 | async-start | bytes 4194304
  267.0 12.6 %slice-start.1 = ((s8[6291456]{0:T(1024)(128)(4,1)}), s8[4194304]{0:T(1024)(128)(4,1)S(1)}, s32[]{:S(2)}) async-start(s8[6291456]{0:T(1024)(128)(4,1)} %bitcast.107), calls=%async_computation.3 | async-start | bytes 8388608
  287.3 3.3 copy-start.1
Sparse Core Ops, SparseCore 0:
  124.1 61.6 all-gather.4
  297.2 82.5 all-gather.6
